TPU v7x, 32 devices: a whole 2x2x4 slice. The times are simulated.
32 devices in a mesh: pat: 2 (over y), slab: 4 (over z), phase: 2 (over x), enc: 2 (over core).
Axes of the slice: x: 2, y: 2, z: 4, core: 2. Of those that a mesh axis runs over, the one named last changes fastest.
Arguments:
- kspace_data: bfloat16 [4, 2, 4, 96, 64, 192], P('pat', 'phase', 'enc', 'slab'), parts along dimension 0, may hold values from -6 to 6
- coil_maps: bfloat16 [4, 24, 4, 64, 192], P('pat', None, None, 'slab'), parts along dimension 0, may hold values from -1 to 1
- sampling: int32 [2, 4, 128, 192], P('phase', 'enc', 'pat'), parts along dimension 2, may hold values 0 or 1
Outputs:
- image_estimate: float32 [4, 2, 4, 4, 64, 192], P('pat', 'phase', 'enc', None, 'slab'), parts along dimension 0
- residual: float32 [4, 2, 4, 96, 64, 192], P('pat', 'phase', 'enc', 'slab'), parts along dimension 0
There are 2 independent parts, one for each index of `pat`. A program takes and returns all parts, laid end to end along the dimension named above; each array names one. Nothing has to cross between parts.
All inputs are finite; a program needn't handle non-finite values. No bound on the sum of `sampling` on one device may be relied on, other than what follows from the above.
Results may differ from a plain program's by a relative error of at most 0.0046.
Values may be sent and summed in bfloat16 or wider, within the bound.
A program may use at most 64 MiB of HBM per device.

v0:
```python
import math

import jax
import jax.numpy as jnp
from jax import lax
from jax.sharding import PartitionSpec as P

ITERS = 2


tv_weight = 0.15
smoothing = 0.6


def with_halo(value, sides, width):
    for axis, dim in sides:
        size, length = (lax.axis_size(axis), value.shape[dim])
        up = [(i, (i + 1) % size) for i in range(size)]
        down = [(j, i) for i, j in up]
        last = lax.slice_in_dim(value, length - width, length, axis=dim)
        first = lax.slice_in_dim(value, 0, width, axis=dim)
        before = lax.ppermute(last, axis, up)
        after = lax.ppermute(first, axis, down)
        value = jnp.concatenate([before, value, after], axis=dim)
    return value


def dft_table(length, direction):
    counter = jnp.arange(length, dtype=jnp.int32)
    product = counter[:, None] * counter[None, :] % length
    angle = product.astype(jnp.float32) * (2.0 * math.pi / length)
    factor = 1.0 / math.sqrt(length)
    return (
        (jnp.cos(angle) * factor).astype(jnp.bfloat16),
        (direction * jnp.sin(angle) * factor).astype(jnp.bfloat16),
    )


def along_rows(real_part, imag_part, table):
    cosine, sine = table
    real_out = jnp.matmul(real_part, cosine, preferred_element_type=jnp.float32) - jnp.matmul(
        imag_part, sine, preferred_element_type=jnp.float32
    )
    imag_out = jnp.matmul(real_part, sine, preferred_element_type=jnp.float32) + jnp.matmul(
        imag_part, cosine, preferred_element_type=jnp.float32
    )
    return (real_out, imag_out)


def along_depth(real_part, imag_part, table):
    cosine, sine = table
    real_out = jnp.einsum(
        "...zy,zw->...wy", real_part, cosine, preferred_element_type=jnp.float32
    ) - jnp.einsum("...zy,zw->...wy", imag_part, sine, preferred_element_type=jnp.float32)
    imag_out = jnp.einsum(
        "...zy,zw->...wy", real_part, sine, preferred_element_type=jnp.float32
    ) + jnp.einsum("...zy,zw->...wy", imag_part, cosine, preferred_element_type=jnp.float32)
    return (real_out, imag_out)


def coil_product(coil_real, coil_imag, real_in, imag_in, column_fwd):
    prod_real = (coil_real * real_in - coil_imag * imag_in).astype(jnp.bfloat16)
    prod_imag = (coil_real * imag_in + coil_imag * real_in).astype(jnp.bfloat16)
    mid_real, mid_imag = along_rows(prod_real, prod_imag, column_fwd)
    return jnp.stack([mid_real, mid_imag]).astype(jnp.bfloat16)


def body(kspace_data, coil_maps, sampling):
    phases = kspace_data.shape[1]
    encodings = kspace_data.shape[2]
    coils = coil_maps.shape[1]
    readout = coil_maps.shape[2]
    zdepth = coil_maps.shape[3]
    lines = coil_maps.shape[4]
    slices = kspace_data.shape[4]
    column_fwd = dft_table(lines, -1.0)
    depth_fwd = dft_table(slices, -1.0)
    column_inv = dft_table(lines, 1.0)
    depth_inv = dft_table(slices, 1.0)
    coil_real = coil_maps[0].astype(jnp.float32)
    coil_imag = coil_maps[1].astype(jnp.float32)
    sampled = sampling.astype(jnp.float32)[None, :, :, None]
    residual = -(kspace_data.astype(jnp.float32) * sampled)
    image_estimate = jnp.zeros((2, phases, encodings, readout, zdepth, lines), jnp.float32)
    row_count = kspace_data.shape[3]
    coil_rows = lax.all_to_all(
        coil_maps.reshape(2, coils * readout, zdepth, lines),
        "slab",
        split_axis=1,
        concat_axis=2,
        tiled=True,
    )
    row_columns = (
        lax.axis_index("slab") * row_count + jnp.arange(row_count, dtype=jnp.int32)
    ) % readout
    for iteration in range(ITERS):
        low = residual.astype(jnp.bfloat16)
        inv_real, inv_imag = along_depth(low[0], low[1], depth_inv)
        partial_rows = jnp.stack([inv_real, inv_imag]).astype(jnp.bfloat16)
        portion = lax.all_to_all(partial_rows, "slab", split_axis=4, concat_axis=3, tiled=True)
        shaped = portion.reshape(
            2,
            portion.shape[1],
            portion.shape[2],
            coils,
            readout,
            portion.shape[4],
            portion.shape[5],
        )
        fine_real, fine_imag = along_rows(shaped[0], shaped[1], column_inv)
        grad_real = jnp.sum(coil_real * fine_real + coil_imag * fine_imag, axis=2)
        grad_imag = jnp.sum(coil_real * fine_imag - coil_imag * fine_real, axis=2)
        adjoint = jnp.stack([grad_real, grad_imag])
        padded = with_halo(image_estimate, (("phase", 1),), 1)
        difference = padded[:, 1:] - padded[:, :-1]
        modulus = difference[0] * difference[0] + difference[1] * difference[1]
        weights = difference / jnp.sqrt(modulus + smoothing * smoothing)[None]
        gradient = adjoint + tv_weight * (weights[:, :-1] - weights[:, 1:])
        grad_local = jnp.sum(gradient * gradient)
        grad_sq = lax.psum(grad_local, ("slab", "phase", "enc"))
        low_grad = gradient.astype(jnp.bfloat16)
        picked = jnp.take(
            lax.all_gather(low_grad, "slab", axis=4, tiled=True), row_columns, axis=3
        ).astype(jnp.float32)
        local_coils = coil_rows.astype(jnp.float32)
        mid = coil_product(local_coils[0], local_coils[1], picked[0], picked[1], column_fwd)
        out_real, out_imag = along_depth(mid[0], mid[1], depth_fwd)
        spectrum = jnp.stack([out_real, out_imag])
        spectrum = spectrum * sampled
        spec_local = jnp.sum(spectrum * spectrum)
        spec_sq = lax.psum(spec_local, ("slab", "phase", "enc"))
        alpha = grad_sq / (spec_sq + 4.0 * tv_weight / smoothing * grad_sq + 1e-06)
        image_estimate = image_estimate - alpha * gradient
        residual = residual - alpha * spectrum
    return (image_estimate, residual)


def solution(mesh):
    in_specs = (
        P("pat", "phase", "enc", "slab", None, None),
        P("pat", None, None, "slab", None),
        P("phase", "enc", "pat", None),
    )
    out_specs = (
        P("pat", "phase", "enc", None, "slab", None),
        P("pat", "phase", "enc", "slab", None, None),
    )
    return jax.shard_map(body, mesh=mesh, in_specs=in_specs, out_specs=out_specs, check_vma=False)
```

profile of v0, /device:TPU:0, one launch (start us, length us, event | category | flops | bytes accessed | tf_op | source)
XLA Modules:
  0.0 373.1 jit_solution(6726968447215893808)
XLA Ops:
  0.7 2.9 copy.52
  3.6 6.3 %all-to-all-start.1 = ((bf16[2,96,16,192]{3,2,0,1:T(8,128)(2,1)}), bf16[2,96,16,192]{3,2,0,1:T(8,128)(2,1)}, u32[]{:S(2)}, u32[]{:S(2)}) async-start(bf16[2,96,16,192]{3,2,0,1:T(8,128)(2,1)} %bitcast.243), calls=%async_computation.1 | async-start | bytes 3145728 | tf_op jit(solution)/shard_map/all_to_all | solution.py:86
  9.9 0.9 fusion
  12.8 0.7 fusion.5
  14.2 3.4 copy.50
  17.6 29.4 %all-to-all-done.1 = bf16[2,96,16,192]{3,2,0,1:T(8,128)(2,1)} async-done(((bf16[2,96,16,192]{3,2,0,1:T(8,128)(2,1)}), bf16[2,96,16,192]{3,2,0,1:T(8,128)(2,1)}, u32[]{:S(2)}, u32[]{:S(2)}) %all-to-all-start.1) | async-done | bytes 1179680 | tf_op jit(solution)/shard_map/all_to_all | solution.py:86
  47.0 5.1 %all-to-all-start = ((bf16[2,1,2,24,64,192]{5,3,2,1,0,4:T(8,128)(2,1)}), bf16[2,1,2,24,64,192]{5,3,2,1,0,4:T(8,128)(2,1)}, u32[]{:S(2)}, u32[]{:S(2)}) async-start(bf16[2,1,2,24,64,192]{5,3,2,1,0,4:T(8,128)(2,1)} %copy.50), calls=%async_computation | async-start | bytes 6291456 | tf_op jit(solution)/shard_map/all_to_all | solution.py:100
  52.1 0.7 broadcast_in_dim.8
  52.8 1.5 collective-permute-start
  54.9 1.8 bitcast_convert_fusion.1
  56.7 5.5 %collective-permute-done = f32[2,1,2,4,16,192]{5,4,3,2,0,1:T(8,128)S(1)} collective-permute-done((f32[2,1,2,4,16,192]{5,4,3,2,0,1:T(8,128)}, f32[2,1,2,4,16,192]{5,4,3,2,0,1:T(8,128)S(1)}, u32[]{:S(2)}, u32[]{:S(2)}) %collective-permute-start) | collective-permute-done | bytes 196640 | tf_op jit(solution)/shard_map/ppermute | solution.py:23
  62.2 3.9 %collective-permute-done.1 = f32[2,1,2,4,16,192]{5,4,3,2,0,1:T(8,128)} collective-permute-done((f32[2,1,2,4,16,192]{5,4,3,2,0,1:T(8,128)}, f32[2,1,2,4,16,192]{5,4,3,2,0,1:T(8,128)}, u32[]{:S(2)}, u32[]{:S(2)}) %collective-permute-start.1) | collective-permute-done | bytes 196640 | tf_op jit(solution)/shard_map/ppermute | solution.py:22
  66.1 1.1 fusion.30
  67.2 1.8 fusion.24
  69.0 1.9 convert_bitcast_fusion
  71.3 1.4 copy.53
  72.7 1.3 copy.55
  74.0 48.4 %all-to-all-done = bf16[2,1,2,24,64,192]{5,3,2,1,0,4:T(8,128)(2,1)} async-done(((bf16[2,1,2,24,64,192]{5,3,2,1,0,4:T(8,128)(2,1)}), bf16[2,1,2,24,64,192]{5,3,2,1,0,4:T(8,128)(2,1)}, u32[]{:S(2)}, u32[]{:S(2)}) %all-to-all-start) | async-done | bytes 2359328 | tf_op jit(solution)/shard_map/all_to_all | solution.py:100
  122.4 3.7 copy.96
  126.2 1.3 fusion.57
  127.5 1.3 fusion.66
  128.9 1.4 convolution_subtract_fusion.1
  130.2 2.4 add_reduce_fusion.1
  132.7 16.1 %all_gather.6 = bf16[2,1,2,4,64,192]{5,4,3,2,0,1:T(8,128)(2,1)S(1)} all-gather(bf16[2,1,2,4,16,192]{5,4,3,2,0,1:T(8,128)(2,1)S(1)} %get-tuple-element.19), channel_id=1, replica_groups=mesh['pat'=2,'slab'=4,'phase'=2,'enc'=2] {'slab'}, dimensions={4}, use_global_device_ids=true | all-gather | bytes 491520 | tf_op jit(solution)/shard_map/all_gather | solution.py:123
  148.8 2.5 gather_fusion
  151.3 2.5 fusion.2
  154.2 1.3 add_convert_fusion.4
  155.4 1.3 fusion.20
  156.7 1.3 fusion.22
  158.0 1.3 subtract_convert_fusion.3
  160.7 1.3 add_convert_fusion.3
  162.7 0.7 add_bitcast_fusion.1
  163.4 2.2 multiply_reduce_fusion.1
  166.3 30.5 %all-reduce.3 = (f32[]{:T(128)}, f32[]{:T(128)}) all-reduce(f32[]{:T(128)} %multiply_reduce_fusion.3, f32[]{:T(128)} %multiply_reduce_fusion.1), channel_id=1, replica_groups=mesh['pat'=2,'slab'=4,'phase'=2,'enc'=2] {'slab','phase','enc'}, use_global_device_ids=true, to_apply=%region_3.4 | all-reduce | flops 2 | bytes 16 | tf_op jit(solution)/shard_map/psum | solution.py:120
  198.8 3.6 fusion.3
  203.8 0.7 fusion.6
  204.5 0.7 fusion.7
  205.8 3.4 copy.60
  209.3 4.6 %all-to-all-start.2 = ((bf16[2,1,2,24,64,192]{5,3,2,1,0,4:T(8,128)(2,1)}), bf16[2,1,2,24,64,192]{5,3,2,1,0,4:T(8,128)(2,1)}, u32[]{:S(2)}, u32[]{:S(2)}) async-start(bf16[2,1,2,24,64,192]{5,3,2,1,0,4:T(8,128)(2,1)} %copy.60), calls=%async_computation.2 | async-start | bytes 6291456 | tf_op jit(solution)/shard_map/all_to_all | solution.py:100
  214.0 2.0 collective-permute-start.3
  216.0 7.2 %collective-permute-done.2 = f32[2,1,2,4,16,192]{5,4,3,2,0,1:T(8,128)S(1)} collective-permute-done((f32[2,1,2,4,16,192]{5,4,3,2,0,1:T(8,128)S(1)}, f32[2,1,2,4,16,192]{5,4,3,2,0,1:T(8,128)S(1)}, u32[]{:S(2)}, u32[]{:S(2)}) %collective-permute-start.2) | collective-permute-done | bytes 196640 | tf_op jit(solution)/shard_map/ppermute | solution.py:23
  223.2 4.5 %collective-permute-done.3 = f32[2,1,2,4,16,192]{5,4,3,2,0,1:T(8,128)S(1)} collective-permute-done((f32[2,1,2,4,16,192]{5,4,3,2,0,1:T(8,128)S(1)}, f32[2,1,2,4,16,192]{5,4,3,2,0,1:T(8,128)S(1)}, u32[]{:S(2)}, u32[]{:S(2)}) %collective-permute-start.3) | collective-permute-done | bytes 196640 | tf_op jit(solution)/shard_map/ppermute | solution.py:22
  227.9 0.9 broadcast_divide_fusion
  228.8 56.1 %all-to-all-done.2 = bf16[2,1,2,24,64,192]{5,3,2,1,0,4:T(8,128)(2,1)} async-done(((bf16[2,1,2,24,64,192]{5,3,2,1,0,4:T(8,128)(2,1)}), bf16[2,1,2,24,64,192]{5,3,2,1,0,4:T(8,128)(2,1)}, u32[]{:S(2)}, u32[]{:S(2)}) %all-to-all-start.2) | async-done | bytes 2359328 | tf_op jit(solution)/shard_map/all_to_all | solution.py:100
  285.0 3.7 copy.95
  288.9 1.3 fusion.54
  290.2 1.3 fusion.63
  291.5 1.4 convolution_subtract_fusion
  293.4 2.4 add_reduce_fusion
  295.8 0.8 fusion.244
  296.6 16.5 %all_gather.7 = bf16[2,1,2,4,64,192]{5,4,3,2,0,1:T(8,128)(2,1)} all-gather(bf16[2,1,2,4,16,192]{5,4,3,2,0,1:T(8,128)(2,1)S(1)} %get-tuple-element.17), channel_id=1, replica_groups=mesh['pat'=2,'slab'=4,'phase'=2,'enc'=2] {'slab'}, dimensions={4}, use_global_device_ids=true | all-gather | bytes 491520 | tf_op jit(solution)/shard_map/all_gather | solution.py:123
  313.1 3.6 gather_fusion.1
  316.7 2.6 fusion.1
  319.5 1.3 add_convert_fusion.1
  320.8 1.3 fusion.14
  322.1 1.3 fusion.16
  323.4 1.3 subtract_convert_fusion
  326.1 1.3 add_convert_fusion
  328.1 0.7 add_bitcast_fusion
  328.8 1.0 copy-done.6
  329.8 2.2 multiply_reduce_fusion
  332.7 30.1 %all-reduce.2 = (f32[]{:T(128)}, f32[]{:T(128)}) all-reduce(f32[]{:T(128)} %multiply_reduce_fusion.2, f32[]{:T(128)} %multiply_reduce_fusion), channel_id=1, replica_groups=mesh['pat'=2,'slab'=4,'phase'=2,'enc'=2] {'slab','phase','enc'}, use_global_device_ids=true, to_apply=%region_9.11 | all-reduce | flops 2 | bytes 16 | tf_op jit(solution)/shard_map/psum | solution.py:120
  364.7 7.4 %multiply_subtract_fusion = f32[2,1,2,24,64,192]{5,4,3,2,1,0:T(8,128)} fusion(f32[1,1,2,24,64,192]{5,4,3,2,1,0:T(8,128)} %copy-done.7, f32[1,1,2,24,64,192]{5,4,3,2,1,0:T(8,128)} %copy-done.6, f32[]{:T(128)S(6)} %div.33, f32[2,64,192]{2,1,0:T(8,128)S(1)} %convert_bitcast_fusion.1, f32[1,1,2,24,64,192]{5,4,3,2,1,0:T(8,128)} %copy-done, ...), kind=kLoop, calls=%fused_computation.4 | loop fusion | flops 12976128 | bytes 16613384 | tf_op jit(solution)/shard_map/sub | solution.py:134
  372.2 0.7 subtract_bitcast_fusion.2
  (61 shorter events, 12.9 us)
Async XLA Ops:
  0.6 9.3 %copy-start.16 = (s32[1,2,64,192]{3,2,1,0:T(8,128)S(1)}, s32[1,2,64,192]{3,2,1,0:T(8,128)}, u32[]{:S(2)}) copy-start(s32[1,2,64,192]{3,2,1,0:T(8,128)} %param.7) | copy-start | bytes 294916
  0.6 9.3 %copy-start.5 = (bf16[2,1,2,24,64,192]{5,4,3,2,1,0:T(8,128)(2,1)S(1)}, bf16[2,1,2,24,64,192]{5,4,3,2,1,0:T(8,128)(2,1)}, u32[]{:S(2)}) copy-start(bf16[2,1,2,24,64,192]{5,4,3,2,1,0:T(8,128)(2,1)} %param.5) | copy-start | bytes 7077892
  3.6 43.4 %all-to-all-start.1 = ((bf16[2,96,16,192]{3,2,0,1:T(8,128)(2,1)}), bf16[2,96,16,192]{3,2,0,1:T(8,128)(2,1)}, u32[]{:S(2)}, u32[]{:S(2)}) async-start(bf16[2,96,16,192]{3,2,0,1:T(8,128)(2,1)} %bitcast.243), calls=%async_computation.1 | async-start | bytes 3145728 | tf_op jit(solution)/shard_map/all_to_all | solution.py:86
  47.0 75.4 %all-to-all-start = ((bf16[2,1,2,24,64,192]{5,3,2,1,0,4:T(8,128)(2,1)}), bf16[2,1,2,24,64,192]{5,3,2,1,0,4:T(8,128)(2,1)}, u32[]{:S(2)}, u32[]{:S(2)}) async-start(bf16[2,1,2,24,64,192]{5,3,2,1,0,4:T(8,128)(2,1)} %copy.50), calls=%async_computation | async-start | bytes 6291456 | tf_op jit(solution)/shard_map/all_to_all | solution.py:100
  52.8 9.4 %collective-permute-start = (f32[2,1,2,4,16,192]{5,4,3,2,0,1:T(8,128)}, f32[2,1,2,4,16,192]{5,4,3,2,0,1:T(8,128)S(1)}, u32[]{:S(2)}, u32[]{:S(2)}) collective-permute-start(f32[2,1,2,4,16,192]{5,4,3,2,0,1:T(8,128)} %broadcast_in_dim.8), channel_id=1, source_target_pairs={{2,0},{0,2},{3,1},{1,3},{6,4},{4,6},{7,5},{5,7},{10,8},{8,10},{11,... | collective-permute-start | bytes 589832 | tf_op jit(solution)/shard_map/ppermute | solution.py:23
  54.3 11.8 %collective-permute-start.1 = (f32[2,1,2,4,16,192]{5,4,3,2,0,1:T(8,128)}, f32[2,1,2,4,16,192]{5,4,3,2,0,1:T(8,128)}, u32[]{:S(2)}, u32[]{:S(2)}) collective-permute-start(f32[2,1,2,4,16,192]{5,4,3,2,0,1:T(8,128)} %broadcast_in_dim.8), channel_id=1, source_target_pairs={{0,2},{2,0},{1,3},{3,1},{4,6},{6,4},{5,7},{7,5},{8,10},{10,8},{9,1... | collective-permute-start | bytes 589832 | tf_op jit(solution)/shard_map/ppermute | solution.py:22
  56.7 73.6 %copy-start.1 = (f32[24,4,16,192]{3,2,1,0:T(8,128)}, f32[24,4,16,192]{3,2,1,0:T(8,128)S(1)}, u32[]{:S(2)}) copy-start(f32[24,4,16,192]{3,2,1,0:T(8,128)S(1)} %get-tuple-element.31) | copy-start | bytes 3538948
  56.7 73.6 %copy-start.3 = (f32[24,4,16,192]{3,2,1,0:T(8,128)}, f32[24,4,16,192]{3,2,1,0:T(8,128)S(1)}, u32[]{:S(2)}) copy-start(f32[24,4,16,192]{3,2,1,0:T(8,128)S(1)} %get-tuple-element.32) | copy-start | bytes 3538948
  130.2 2.4 copy-start.15
  151.3 2.5 copy-start.8
  151.3 2.8 copy-start.10
  163.4 2.2 copy-start
  209.3 75.7 %all-to-all-start.2 = ((bf16[2,1,2,24,64,192]{5,3,2,1,0,4:T(8,128)(2,1)}), bf16[2,1,2,24,64,192]{5,3,2,1,0,4:T(8,128)(2,1)}, u32[]{:S(2)}, u32[]{:S(2)}) async-start(bf16[2,1,2,24,64,192]{5,3,2,1,0,4:T(8,128)(2,1)} %copy.60), calls=%async_computation.2 | async-start | bytes 6291456 | tf_op jit(solution)/shard_map/all_to_all | solution.py:100
  214.0 9.2 %collective-permute-start.2 = (f32[2,1,2,4,16,192]{5,4,3,2,0,1:T(8,128)S(1)}, f32[2,1,2,4,16,192]{5,4,3,2,0,1:T(8,128)S(1)}, u32[]{:S(2)}, u32[]{:S(2)}) collective-permute-start(f32[2,1,2,4,16,192]{5,4,3,2,0,1:T(8,128)S(1)} %multiply_subtract_fusion.2), channel_id=1, source_target_pairs={{2,0},{0,2},{3,1},{1,3},{6,4},{4,6},{7,5},{5,7},{10,8},{8,10},{11,... | collective-permute-start | bytes 589832 | tf_op jit(solution)/shard_map/ppermute | solution.py:23
  214.0 13.7 %collective-permute-start.3 = (f32[2,1,2,4,16,192]{5,4,3,2,0,1:T(8,128)S(1)}, f32[2,1,2,4,16,192]{5,4,3,2,0,1:T(8,128)S(1)}, u32[]{:S(2)}, u32[]{:S(2)}) collective-permute-start(f32[2,1,2,4,16,192]{5,4,3,2,0,1:T(8,128)S(1)} %multiply_subtract_fusion.2), channel_id=1, source_target_pairs={{0,2},{2,0},{1,3},{3,1},{4,6},{6,4},{5,7},{7,5},{8,10},{10,8},{9,1... | collective-permute-start | bytes 589832 | tf_op jit(solution)/shard_map/ppermute | solution.py:22
  291.5 1.4 copy-start.2
  291.5 1.9 copy-start.4
  293.4 2.4 copy-start.14
  316.7 2.6 copy-start.9
  316.7 2.8 copy-start.11
  328.0 1.7 copy-start.6
  329.8 2.3 copy-start.7
  329.8 2.3 copy-start.12
  364.7 7.4 %copy-start.13 = (f32[2,1,2,4,16,192]{5,4,3,2,0,1:T(8,128)S(1)}, f32[2,1,2,4,16,192]{5,4,3,2,0,1:T(8,128)}, u32[]{:S(2)}) copy-start(f32[2,1,2,4,16,192]{5,4,3,2,0,1:T(8,128)} %get-tuple-element.18) | copy-start | bytes 589828
where the time goes:
time: 379 us; the launch traced here: 373 us
  waiting for transfers between devices  155 us (41%)
  blocking collectives  93.2 us (25%)
  other arithmetic  35.8 us (9%)
  matrix products  34.2 us (9%)
  local copies, waits for them, and re-layouts  29.6 us (8%)
  starting transfers between devices  20.2 us (5%)
  between operations  5.15 us (1%)
    all_to_all x2, waiting for transfers between devices, body(): lax.all_to_all(partial_rows, 'slab', split_axis=4, concat_axis=3, tiled=T...  105 us
    psum x2, blocking collectives, body(): grad_sq = lax.psum(grad_local, ('slab', 'phase', 'enc'))  60.6 us
    all_gather x2, blocking collectives, body(): lax.all_gather(low_grad, 'slab', axis=4, tiled=True)  32.6 us
    all_to_all x1, waiting for transfers between devices, body(): lax.all_to_all(coil_maps.reshape(2, coils * readout, zdepth, lines), 'sla...  29.4 us
    ppermute x2, waiting for transfers between devices, with_halo(): after = lax.ppermute(first, axis, down)  12.6 us
    all_to_all x2, starting transfers between devices, body(): lax.all_to_all(partial_rows, 'slab', split_axis=4, concat_axis=3, tiled=T...  9.75 us
    ppermute x2, waiting for transfers between devices, with_halo(): before = lax.ppermute(last, axis, up)  8.38 us
  transfers between devices with their start and end apart: 7, of which 7 were waited for; matrix products, arithmetic and copies ran while one was open for 5% of the time, Pallas kernels for 0%

commit v1 on v0

--- a/solution.py
+++ b/solution.py
@@ -1,8 +1,12 @@
+import functools
 import math
 
 import jax
 import jax.numpy as jnp
+import numpy as np
 from jax import lax
+from jax.experimental import pallas as pl
+from jax.experimental.pallas import tpu as pltpu
 from jax.sharding import PartitionSpec as P
 
 ITERS = 2
@@ -135,6 +139,405 @@
     return (image_estimate, residual)
 
 
+MESH = pl.DeviceIdType.MESH
+LAG = 3
+
+
+def host_table(length):
+    counter = np.arange(length)
+    angle = (counter[:, None] * counter[None, :] % length).astype(np.float32) * np.float32(
+        2.0 * math.pi / length
+    )
+    factor = np.float32(1.0 / math.sqrt(length))
+    return (
+        (np.cos(angle) * factor).astype(jnp.bfloat16),
+        (np.sin(angle) * factor).astype(jnp.bfloat16),
+    )
+
+
+def fused(sizes, k_ref, coil_ref, samp_ref, cy_ref, sy_ref, ti_ref, tf_ref, img_ref, res_ref,
+          rows_ref, mask_ref, q_ref, e_ref, rs_ref, rr_ref, own_ref, ag_ref, g_ref, tv_ref,
+          ar_ref, gg_ref, ee_ref,
+          own_sem, cz_send, cz_recv, cx_send, cx_recv, cc_send, cc_recv,
+          rs_send, rs_recv, ag_send, ag_recv, tv_send, tv_recv, ar_send, ar_recv):
+    n, nphase, nenc = sizes
+    readout, depth = coil_ref.shape[2], coil_ref.shape[3]
+    encs = k_ref.shape[2]
+    slices, lines = k_ref.shape[4], k_ref.shape[5]
+    coils = k_ref.shape[3] // readout
+    pieces = encs * readout
+    me = lax.axis_index("slab")
+    ph = lax.axis_index("phase")
+    en = lax.axis_index("enc")
+    f32, bf16 = jnp.float32, jnp.bfloat16
+
+    def wrap(value, size):
+        return lax.rem(value + size, size)
+
+    offsets = [
+        (a, b, c)
+        for a in range(n)
+        for b in range(nphase)
+        for c in range(nenc)
+        if (a, b, c) != (0, 0, 0)
+    ]
+
+    def rel(a, b, c):
+        return {"slab": wrap(me + a, n), "phase": wrap(ph + b, nphase), "enc": wrap(en + c, nenc)}
+
+    def remote(src, dst, send, recv, where):
+        return pltpu.make_async_remote_copy(
+            src_ref=src, dst_ref=dst, send_sem=send, recv_sem=recv, device_id=where,
+            device_id_type=MESH,
+        )
+
+    barrier = pltpu.get_barrier_semaphore()
+    for off in offsets:
+        pl.semaphore_signal(barrier, inc=1, device_id=rel(*off), device_id_type=MESH)
+    pl.semaphore_wait(barrier, len(offsets))
+
+    quarter = ph * nenc + en
+    across = wrap(ph + 1, nphase) * nenc + en
+
+    def coil_z(k):
+        to = wrap(me + k, n)
+        return remote(
+            coil_ref.at[:, pl.ds(to * coils, coils), quarter], rows_ref.at[me, :, :, quarter],
+            cz_send.at[k - 1], cz_recv.at[k - 1], rel(k, 0, 0),
+        )
+
+    def coil_z_in(k):
+        frm = wrap(me - k, n)
+        return remote(
+            coil_ref.at[:, pl.ds(0, coils), quarter], rows_ref.at[frm, :, :, quarter],
+            cz_send.at[k - 1], cz_recv.at[k - 1], rel(k, 0, 0),
+        )
+
+    def coil_x(k, which):
+        at = rows_ref.at[wrap(me - k, n), :, :, which]
+        return remote(at, at, cx_send.at[k - 1], cx_recv.at[k - 1], rel(0, 1, 0))
+
+    def coil_c(k, which, s):
+        at = rows_ref.at[wrap(me - k, n), :, :, which]
+        return remote(at, at, cc_send.at[s, k - 1], cc_recv.at[s, k - 1], rel(0, 0, 1))
+
+    for k in range(1, n):
+        coil_z(k).start()
+    mine = pltpu.make_async_copy(
+        coil_ref.at[:, pl.ds(me * coils, coils)], rows_ref.at[me], own_sem
+    )
+    mine.start()
+
+    mask_ref[...] = samp_ref[0].astype(f32)
+    gg_ref[...] = jnp.zeros_like(gg_ref)
+    ee_ref[...] = jnp.zeros_like(ee_ref)
+
+    def transform(i, alpha):
+        e, x = i // readout, lax.rem(i, readout)
+        mask = mask_ref[e]
+        mids = []
+        for c in range(coils):
+            r = c * readout + x
+            parts = []
+            for ri in range(2):
+                value = -(k_ref[ri, 0, e, r].astype(f32) * mask)
+                if alpha is not None:
+                    value = value - alpha * e_ref[i, c, ri]
+                    res_ref[ri, 0, e, r] = value
+                parts.append(value.astype(bf16))
+            stacked = jnp.concatenate(parts, axis=0)
+            mids.append(
+                jnp.dot(ti_ref[...], stacked, preferred_element_type=f32).astype(bf16)
+            )
+        mid = jnp.concatenate(mids, axis=0)
+        a = jnp.dot(mid, cy_ref[...], preferred_element_type=f32)
+        b = jnp.dot(mid, sy_ref[...], preferred_element_type=f32)
+        for c in range(coils):
+            lo = 2 * slices * c
+            hi = lo + slices
+            q_ref[i, c, 0] = a[lo : lo + slices] - b[hi : hi + slices]
+            q_ref[i, c, 1] = b[lo : lo + slices] + a[hi : hi + slices]
+
+    def coil_of(c, x):
+        return [
+            jnp.concatenate([rows_ref[b, ri, c, x] for b in range(n)], axis=0).astype(f32)
+            for ri in range(2)
+        ]
+
+    def rs_copy(it, i, k):
+        return remote(
+            rs_ref.at[it, i, wrap(me + k, n)], rr_ref.at[it, i, k - 1],
+            rs_send.at[i, k - 1], rs_recv.at[i, k - 1], rel(k, 0, 0),
+        )
+
+    def ag_copy(it, i, k):
+        return remote(
+            ag_ref.at[it, i, me], ag_ref.at[it, i, me],
+            ag_send.at[i, k - 1], ag_recv.at[i, k - 1], rel(k, 0, 0),
+        )
+
+    def ag_in(it, i, k):
+        at = ag_ref.at[it, i, wrap(me - k, n)]
+        return remote(at, at, ag_send.at[i, k - 1], ag_recv.at[i, k - 1], rel(k, 0, 0))
+
+    def tv_copy(i):
+        return remote(g_ref.at[0, i], tv_ref.at[i], tv_send.at[i], tv_recv.at[i], rel(0, 1, 0))
+
+    def combine(it, i):
+        x = lax.rem(i, readout)
+        pr = jnp.zeros((slices, lines), f32)
+        pi = jnp.zeros((slices, lines), f32)
+        for c in range(coils):
+            cr, ci = coil_of(c, x)
+            qr, qi = q_ref[i, c, 0], q_ref[i, c, 1]
+            pr += cr * qr + ci * qi
+            pi += cr * qi - ci * qr
+        for b in range(n):
+            for ri, part in enumerate((pr, pi)):
+                cut = part[b * depth : (b + 1) * depth]
+                own_ref[i, b, ri] = cut
+                rs_ref[it, i, b, ri] = cut.astype(bf16)
+        for k in range(1, n):
+            rs_copy(it, i, k).start()
+
+    def reduce(it, i, alpha):
+        for k in range(1, n):
+            rs_copy(it, i, k).wait_recv()
+        grads = []
+        for ri in range(2):
+            total = own_ref[i, me, ri]
+            for k in range(1, n):
+                total = total + rr_ref[it, i, k - 1, ri].astype(f32)
+            grads.append(total)
+        if it > 0:
+            tv_copy(i).wait_recv()
+            dr = -alpha * (tv_ref[i, 0] - g_ref[0, i, 0])
+            di = -alpha * (tv_ref[i, 1] - g_ref[0, i, 1])
+            scale = (-2.0 * tv_weight) / jnp.sqrt(dr * dr + di * di + smoothing * smoothing)
+            grads = [grads[0] + dr * scale, grads[1] + di * scale]
+        for ri in range(2):
+            g_ref[it, i, ri] = grads[ri]
+            ag_ref[it, i, me, ri] = grads[ri].astype(bf16)
+        gg_ref[...] += grads[0] * grads[0] + grads[1] * grads[1]
+        for k in range(1, n):
+            ag_copy(it, i, k).start()
+        if it == 0:
+            tv_copy(i).start()
+
+    def forward(it, i):
+        e, x = i // readout, lax.rem(i, readout)
+        for k in range(1, n):
+            ag_in(it, i, k).wait_recv()
+        vr, vi = [
+            jnp.concatenate([ag_ref[it, i, b, ri] for b in range(n)], axis=0).astype(f32)
+            for ri in range(2)
+        ]
+        prods = []
+        for c in range(coils):
+            cr, ci = coil_of(c, x)
+            prods.append((cr * vr - ci * vi).astype(bf16))
+            prods.append((cr * vi + ci * vr).astype(bf16))
+        prod = jnp.concatenate(prods, axis=0)
+        a = jnp.dot(prod, cy_ref[...], preferred_element_type=f32)
+        b = jnp.dot(prod, sy_ref[...], preferred_element_type=f32)
+        mask = mask_ref[e]
+        total = jnp.zeros((slices, lines), f32)
+        for c in range(coils):
+            lo = 2 * slices * c
+            hi = lo + slices
+            mid = jnp.concatenate(
+                [
+                    (a[lo : lo + slices] + b[hi : hi + slices]).astype(bf16),
+                    (a[hi : hi + slices] - b[lo : lo + slices]).astype(bf16),
+                ],
+                axis=0,
+            )
+            out = jnp.dot(tf_ref[...], mid, preferred_element_type=f32)
+            er, ei = out[:slices] * mask, out[slices:] * mask
+            e_ref[i, c, 0] = er
+            e_ref[i, c, 1] = ei
+            total += er * er + ei * ei
+        ee_ref[...] += total
+
+    flat = (me * nphase + ph) * nenc + en
+
+    def ar_copy(it, j):
+        return remote(
+            ar_ref.at[it, flat], ar_ref.at[it, flat], ar_send.at[it, j], ar_recv.at[it, j],
+            rel(*offsets[j]),
+        )
+
+    def ar_in(it, j):
+        a, b, c = offsets[j]
+        frm = (wrap(me - a, n) * nphase + wrap(ph - b, nphase)) * nenc + wrap(en - c, nenc)
+        at = ar_ref.at[it, frm]
+        return remote(at, at, ar_send.at[it, j], ar_recv.at[it, j], rel(*offsets[j]))
+
+    def step_size(it):
+        gg = jnp.sum(jnp.sum(gg_ref[...], axis=0, keepdims=True), axis=1, keepdims=True)
+        ee = jnp.sum(jnp.sum(ee_ref[...], axis=0, keepdims=True), axis=1, keepdims=True)
+        row = lax.broadcasted_iota(jnp.int32, ar_ref.shape[2:], 0)
+        ar_ref[it, flat] = jnp.where(row == 0, gg, ee)
+        for j in range(len(offsets)):
+            ar_copy(it, j).start()
+        gg_ref[...] = jnp.zeros_like(gg_ref)
+        ee_ref[...] = jnp.zeros_like(ee_ref)
+        for j in range(len(offsets)):
+            ar_in(it, j).wait_recv()
+        total = ar_ref[it, 0]
+        for s in range(1, n * nphase * nenc):
+            total = total + ar_ref[it, s]
+        gg, ee = total[0:1, 0:1], total[1:2, 0:1]
+        return gg / (ee + 4.0 * tv_weight / smoothing * gg + 1e-06)
+
+    def finish_sends(it):
+        @pl.loop(0, pieces)
+        def _(i):
+            for k in range(1, n):
+                rs_copy(it, i, k).wait_send()
+                ag_copy(it, i, k).wait_send()
+            if it == 0:
+                tv_copy(i).wait_send()
+
+        for j in range(len(offsets)):
+            ar_copy(it, j).wait_send()
+
+    def sweep(it, alpha):
+        @pl.loop(0, pieces + 2 * LAG)
+        def _(s):
+            @pl.when(s < pieces)
+            def _():
+                if it > 0:
+                    transform(s, alpha)
+                combine(it, s)
+
+            @pl.when((s >= LAG) & (s < pieces + LAG))
+            def _():
+                reduce(it, s - LAG, alpha)
+
+            @pl.when(s >= 2 * LAG)
+            def _():
+                forward(it, s - 2 * LAG)
+
+    @pl.loop(0, pieces)
+    def _(i):
+        transform(i, None)
+
+    for k in range(1, n):
+        coil_z_in(k).wait_recv()
+        coil_x(k, quarter).start()
+        coil_c(k, quarter, 0).start()
+    for k in range(1, n):
+        coil_x(k, across).wait_recv()
+        coil_c(k, across, 1).start()
+    mine.wait()
+    partner = wrap(en + 1, nenc)
+    for k in range(1, n):
+        coil_c(k, ph * nenc + partner, 0).wait_recv()
+        coil_c(k, wrap(ph + 1, nphase) * nenc + partner, 1).wait_recv()
+
+    sweep(0, None)
+    alpha0 = step_size(0)
+    finish_sends(0)
+    sweep(1, alpha0)
+    alpha1 = step_size(1)
+
+    for ri in range(2):
+        for i in range(pieces):
+            img_ref[ri, 0, i // readout, i % readout] = (
+                -alpha0 * g_ref[0, i, ri] - alpha1 * g_ref[1, i, ri]
+            )
+
+    @pl.loop(0, pieces)
+    def _(i):
+        e, x = i // readout, lax.rem(i, readout)
+        for c in range(coils):
+            r = c * readout + x
+            for ri in range(2):
+                res_ref[ri, 0, e, r] = res_ref[ri, 0, e, r] - alpha1 * e_ref[i, c, ri]
+
+    finish_sends(1)
+    for k in range(1, n):
+        coil_z(k).wait_send()
+        coil_x(k, quarter).wait_send()
+        coil_c(k, quarter, 0).wait_send()
+        coil_c(k, across, 1).wait_send()
+
+
+def fused_body(shape, kspace_data, coil_maps, sampling):
+    n, nphase, nenc = shape["slab"], shape["phase"], shape["enc"]
+    encs, row_count, slices, lines = kspace_data.shape[2:]
+    readout, depth = coil_maps.shape[2:4]
+    coils = row_count // readout
+    pieces = encs * readout
+    group = n * nphase * nenc
+    cy, sy = host_table(lines)
+    cz, sz = host_table(slices)
+    inv = np.block([[cz, -sz], [sz, cz]])
+    fwd = np.block([[cz, sz], [-sz, cz]])
+    f32, bf16 = jnp.float32, jnp.bfloat16
+    dma = pltpu.SemaphoreType.DMA
+    vmem = pl.BlockSpec(memory_space=pltpu.VMEM)
+    return pl.pallas_call(
+        functools.partial(fused, (n, nphase, nenc)),
+        out_shape=[
+            jax.ShapeDtypeStruct((2, 1, encs, readout, depth, lines), f32),
+            jax.ShapeDtypeStruct(kspace_data.shape, f32),
+        ],
+        in_specs=[vmem] * 7,
+        out_specs=[vmem] * 2,
+        scratch_shapes=[
+            pltpu.VMEM((n, 2, coils, readout, depth, lines), bf16),
+            pltpu.VMEM((encs, slices, lines), f32),
+            pltpu.VMEM((pieces, coils, 2, slices, lines), f32),
+            pltpu.VMEM((pieces, coils, 2, slices, lines), f32),
+            pltpu.VMEM((ITERS, pieces, n, 2, depth, lines), bf16),
+            pltpu.VMEM((ITERS, pieces, n - 1, 2, depth, lines), bf16),
+            pltpu.VMEM((pieces, n, 2, depth, lines), f32),
+            pltpu.VMEM((ITERS, pieces, n, 2, depth, lines), bf16),
+            pltpu.VMEM((ITERS, pieces, 2, depth, lines), f32),
+            pltpu.VMEM((pieces, 2, depth, lines), f32),
+            pltpu.VMEM((ITERS, group, 8, 128), f32),
+            pltpu.VMEM((depth, lines), f32),
+            pltpu.VMEM((slices, lines), f32),
+            dma,
+            dma((n - 1,)),
+            dma((n - 1,)),
+            dma((n - 1,)),
+            dma((n - 1,)),
+            dma((2, n - 1)),
+            dma((2, n - 1)),
+            dma((pieces, n - 1)),
+            dma((pieces, n - 1)),
+            dma((pieces, n - 1)),
+            dma((pieces, n - 1)),
+            dma((pieces,)),
+            dma((pieces,)),
+            dma((ITERS, group - 1)),
+            dma((ITERS, group - 1)),
+        ],
+        compiler_params=pltpu.CompilerParams(
+            collective_id=0, has_side_effects=True, vmem_limit_bytes=60 * 1024 * 1024
+        ),
+    )(kspace_data, coil_maps, sampling, jnp.asarray(cy), jnp.asarray(sy), jnp.asarray(inv), jnp.asarray(fwd))
+
+
+def chosen(shape, kspace_data, coil_maps, sampling):
+    readout, depth = coil_maps.shape[2:4]
+    fits = (
+        shape["phase"] == 2
+        and kspace_data.shape[1] == 1
+        and shape["enc"] == 2
+        and readout == shape["phase"] * shape["enc"]
+        and kspace_data.shape[3] % readout == 0
+        and depth % 16 == 0
+        and shape["slab"] > 1
+    )
+    if fits:
+        return fused_body(shape, kspace_data, coil_maps, sampling)
+    return body(kspace_data, coil_maps, sampling)
+
+
 def solution(mesh):
     in_specs = (
         P("pat", "phase", "enc", "slab", None, None),
@@ -145,4 +548,4 @@
         P("pat", "phase", "enc", None, "slab", None),
         P("pat", "phase", "enc", "slab", None, None),
     )
-    return jax.shard_map(body, mesh=mesh, in_specs=in_specs, out_specs=out_specs, check_vma=False)
+    return jax.shard_map(functools.partial(chosen, dict(mesh.shape)), mesh=mesh, in_specs=in_specs, out_specs=out_specs, check_vma=False)

time: 379 us -> 96.7 us (0.26); the launches traced: 373 us -> 96.6 us
  waiting for transfers between devices: 155 us -> 0 us
  blocking collectives: 93.2 us -> 0 us
  Pallas kernels: 0 us -> 88 us
  other arithmetic: 35.8 us -> 0 us
  matrix products: 34.2 us -> 0 us
  local copies, waits for them, and re-layouts: 29.6 us -> 7.97 us
  starting transfers between devices: 20.2 us -> 0 us
  between operations: 5.15 us -> 0.64 us
    all_to_all x3 -> x0, waiting for transfers between devices: 134 us -> none  [the longest x2 105 us: body(): lax.all_to_all(partial_rows, 'slab', split_axis=4, concat_axis=3, tiled=T...]
    pallas_call x0 -> x1, Pallas kernels: none -> 88 us  [fused_body(): pl.pallas_call(functools.partial(fused, (n, nphase, nenc)), out_shape=[ja...]
    psum x2 -> x0, blocking collectives: 60.6 us -> none  [body(): grad_sq = lax.psum(grad_local, ('slab', 'phase', 'enc'))]
    dot_general x32 -> x0, matrix products: 34.2 us -> none  [the longest x4 7.42 us: along_rows(): jnp.matmul(imag_part, cosine, preferred_element_type=jnp.float32)]
    all_gather x2 -> x0, blocking collectives: 32.6 us -> none  [body(): lax.all_gather(low_grad, 'slab', axis=4, tiled=True)]
    ppermute x4 -> x0, waiting for transfers between devices: 21 us -> none  [the longest x2 12.6 us: with_halo(): after = lax.ppermute(first, axis, down)]
    convert_element_type x10 -> x0, other arithmetic: 16.5 us -> none  [the longest x2 5.07 us: body(): picked = jnp.take(lax.all_gather(low_grad, 'slab', axis=4, tiled=True), r...]
    all_to_all x3 -> x0, starting transfers between devices: 16.1 us -> none  [the longest x2 9.75 us: body(): lax.all_to_all(partial_rows, 'slab', split_axis=4, concat_axis=3, tiled=T...]
  transfers between devices with their start and end apart: 7 -> 0, of which waited for: 7 -> 0; matrix products, arithmetic and copies ran while one was open for 5% -> 0% of each run, Pallas kernels for 0% -> 0%
where the time goes in v1:
time: 96.7 us; the launch traced here: 96.6 us
  Pallas kernels  88 us (91%)
  local copies, waits for them, and re-layouts  7.97 us (8%)
    pallas_call x1, Pallas kernels, fused_body(): pl.pallas_call(functools.partial(fused, (n, nphase, nenc)), out_shape=[ja...  88 us
    unnamed x2, local copies, waits for them, and re-layouts  7.97 us

profile of v1, /device:TPU:0, one launch (start us, length us, event | category | flops | bytes accessed | tf_op | source)
XLA Modules:
  0.0 96.6 jit_solution(1789569764207869371)
XLA Ops:
  0.6 88.0 %shard_map.86 = (f32[2,1,2,4,16,192]{5,4,3,2,1,0:T(8,128)}, f32[2,1,2,24,64,192]{5,4,3,2,1,0:T(8,128)}) custom-call(bf16[2,1,2,24,64,192]{5,4,3,2,1,0:T(8,128)(2,1)} %k_ref.1, bf16[2,24,4,16,192]{4,3,2,1,0:T(8,128)(2,1)} %coil_ref.1, s32[1,2,64,192]{3,2,1,0:T(8,128)} %samp_ref.1, bf16[192,192]{1,0:T(8,128)(2,1)} %constant.8.clone.cy_ref, ...), custom_call_target="tpu_custom_call" | custom-call | tf_op jit(solution)/shard_map/pallas_call | solution.py:481
  88.6 1.7 %copy.11 = f32[2,1,2,4,16,192]{5,4,3,2,1,0:T(8,128)} copy(f32[2,1,2,4,16,192]{5,4,3,2,1,0:T(8,128)} %get-tuple-element.4) | data formatting | bytes 393216
  90.3 6.3 %copy.12 = f32[2,1,2,24,64,192]{5,4,3,2,1,0:T(8,128)} copy(f32[2,1,2,24,64,192]{5,4,3,2,1,0:T(8,128)} %get-tuple-element.5) | data formatting | bytes 9437184

commit v2 on v1

--- a/solution.py
+++ b/solution.py
@@ -141,6 +141,10 @@
 
 MESH = pl.DeviceIdType.MESH
 LAG = 3
+HALF = 64
+KEEP = pltpu.VMEM
+LIMIT = 40 * 1024 * 1024
+TAIL_LIMIT = 40 * 1024 * 1024
 
 
 def host_table(length):
@@ -155,10 +159,54 @@
     )
 
 
-def fused(sizes, k_ref, coil_ref, samp_ref, cy_ref, sy_ref, ti_ref, tf_ref, img_ref, res_ref,
-          rows_ref, mask_ref, q_ref, e_ref, rs_ref, rr_ref, own_ref, ag_ref, g_ref, tv_ref,
+def packed(real, imag):
+    full = real.shape[1] - HALF
+    mixed = jnp.concatenate([real[:, full:], imag[:, full:]], axis=1)
+    return [real[:, :full], imag[:, :full], mixed]
+
+
+def unpacked(first, second, mixed):
+    return (
+        jnp.concatenate([first, mixed[:, :HALF]], axis=1),
+        jnp.concatenate([second, mixed[:, HALF:]], axis=1),
+    )
+
+
+def finish(r_ref, e_ref, g_ref, a_ref, img_ref, res_ref, stage_ref, sems):
+    readout = img_ref.shape[3]
+    pieces, coils = e_ref.shape[:2]
+    encs = img_ref.shape[2]
+    alpha0, alpha1 = a_ref[0, 0:1, 0:1], a_ref[1, 0:1, 0:1]
+
+    def out(ri, e):
+        return pltpu.make_async_copy(stage_ref.at[ri, 0, e], res_ref.at[ri, 0, e], sems.at[ri, e])
+
+    for ri in range(2):
+        for e in range(encs):
+            @pl.loop(0, readout)
+            def _(x):
+                for c in range(coils):
+                    r = c * readout + x
+                    stage_ref[ri, 0, e, r] = (
+                        r_ref[ri, 0, e, r] - alpha1 * e_ref[e * readout + x, c, ri]
+                    )
+
+            out(ri, e).start()
+    for i in range(pieces):
+        parts = [-alpha0 * g_ref[0, i, t] - alpha1 * g_ref[1, i, t] for t in range(3)]
+        real, imag = unpacked(*parts)
+        img_ref[0, 0, i // readout, i % readout] = real
+        img_ref[1, 0, i // readout, i % readout] = imag
+    for ri in range(2):
+        for e in range(encs):
+            out(ri, e).wait()
+
+
+def fused(sizes, k_hbm, coil_hbm, samp_hbm, cy_ref, sy_ref, ti_ref, tf_ref, res_ref, e_ref, g_ref,
+          a_ref, k_ref, coil_ref, samp_ref, pack_ref,
+          rows_ref, mask_ref, q_ref, rs_ref, rr_ref, own_ref, ag_ref, tv_ref,
           ar_ref, gg_ref, ee_ref,
-          own_sem, cz_send, cz_recv, cx_send, cx_recv, cc_send, cc_recv,
+          in_sem, cz_send, cz_recv, cx_send, cx_recv, cc_send, cc_recv,
           rs_send, rs_recv, ag_send, ag_recv, tv_send, tv_recv, ar_send, ar_recv):
     n, nphase, nenc = sizes
     readout, depth = coil_ref.shape[2], coil_ref.shape[3]
@@ -194,7 +242,6 @@
     barrier = pltpu.get_barrier_semaphore()
     for off in offsets:
         pl.semaphore_signal(barrier, inc=1, device_id=rel(*off), device_id_type=MESH)
-    pl.semaphore_wait(barrier, len(offsets))
 
     quarter = ph * nenc + en
     across = wrap(ph + 1, nphase) * nenc + en
@@ -202,32 +249,50 @@
     def coil_z(k):
         to = wrap(me + k, n)
         return remote(
-            coil_ref.at[:, pl.ds(to * coils, coils), quarter], rows_ref.at[me, :, :, quarter],
+            pack_ref.at[pl.ds(to * coils, coils)], rows_ref.at[me, :, quarter],
             cz_send.at[k - 1], cz_recv.at[k - 1], rel(k, 0, 0),
         )
 
     def coil_z_in(k):
         frm = wrap(me - k, n)
         return remote(
-            coil_ref.at[:, pl.ds(0, coils), quarter], rows_ref.at[frm, :, :, quarter],
+            pack_ref.at[pl.ds(0, coils)], rows_ref.at[frm, :, quarter],
             cz_send.at[k - 1], cz_recv.at[k - 1], rel(k, 0, 0),
         )
 
     def coil_x(k, which):
-        at = rows_ref.at[wrap(me - k, n), :, :, which]
+        at = rows_ref.at[wrap(me - k, n), :, which]
         return remote(at, at, cx_send.at[k - 1], cx_recv.at[k - 1], rel(0, 1, 0))
 
     def coil_c(k, which, s):
-        at = rows_ref.at[wrap(me - k, n), :, :, which]
+        at = rows_ref.at[wrap(me - k, n), :, which]
         return remote(at, at, cc_send.at[s, k - 1], cc_recv.at[s, k - 1], rel(0, 0, 1))
 
-    for k in range(1, n):
-        coil_z(k).start()
-    mine = pltpu.make_async_copy(
-        coil_ref.at[:, pl.ds(me * coils, coils)], rows_ref.at[me], own_sem
-    )
-    mine.start()
-
+    def load_k(e):
+        return pltpu.make_async_copy(k_hbm.at[:, :, e], k_ref.at[:, :, e], in_sem.at[2 + e])
+
+    load_coil = pltpu.make_async_copy(coil_hbm, coil_ref, in_sem.at[0])
+    load_samp = pltpu.make_async_copy(samp_hbm, samp_ref, in_sem.at[1])
+    load_coil.start()
+    load_samp.start()
+    for e in range(encs):
+        load_k(e).start()
+    load_coil.wait()
+
+    @pl.loop(0, coils * n)
+    def _(c):
+        for t, part in enumerate(packed(coil_ref[0, c, quarter].astype(f32), coil_ref[1, c, quarter].astype(f32))):
+            pack_ref[c, t] = part.astype(bf16)
+
+    @pl.loop(0, coils)
+    def _(c):
+        source = me * coils + c
+        for x in range(readout):
+            parts = packed(coil_ref[0, source, x].astype(f32), coil_ref[1, source, x].astype(f32))
+            for t, part in enumerate(parts):
+                rows_ref[me, c, x, t] = part.astype(bf16)
+
+    load_samp.wait()
     mask_ref[...] = samp_ref[0].astype(f32)
     gg_ref[...] = jnp.zeros_like(gg_ref)
     ee_ref[...] = jnp.zeros_like(ee_ref)
@@ -259,10 +324,10 @@
             q_ref[i, c, 1] = b[lo : lo + slices] + a[hi : hi + slices]
 
     def coil_of(c, x):
-        return [
-            jnp.concatenate([rows_ref[b, ri, c, x] for b in range(n)], axis=0).astype(f32)
-            for ri in range(2)
-        ]
+        return unpacked(*[
+            jnp.concatenate([rows_ref[b, c, x, t] for b in range(n)], axis=0).astype(f32)
+            for t in range(3)
+        ])
 
     def rs_copy(it, i, k):
         return remote(
@@ -292,11 +357,11 @@
             qr, qi = q_ref[i, c, 0], q_ref[i, c, 1]
             pr += cr * qr + ci * qi
             pi += cr * qi - ci * qr
-        for b in range(n):
-            for ri, part in enumerate((pr, pi)):
+        for t, part in enumerate(packed(pr, pi)):
+            for b in range(n):
                 cut = part[b * depth : (b + 1) * depth]
-                own_ref[i, b, ri] = cut
-                rs_ref[it, i, b, ri] = cut.astype(bf16)
+                own_ref[i, b, t] = cut
+                rs_ref[it, i, b, t] = cut.astype(bf16)
         for k in range(1, n):
             rs_copy(it, i, k).start()
 
@@ -304,21 +369,26 @@
         for k in range(1, n):
             rs_copy(it, i, k).wait_recv()
         grads = []
-        for ri in range(2):
-            total = own_ref[i, me, ri]
+        for t in range(3):
+            total = own_ref[i, me, t]
             for k in range(1, n):
-                total = total + rr_ref[it, i, k - 1, ri].astype(f32)
+                total = total + rr_ref[it, i, k - 1, t].astype(f32)
             grads.append(total)
         if it > 0:
             tv_copy(i).wait_recv()
-            dr = -alpha * (tv_ref[i, 0] - g_ref[0, i, 0])
-            di = -alpha * (tv_ref[i, 1] - g_ref[0, i, 1])
-            scale = (-2.0 * tv_weight) / jnp.sqrt(dr * dr + di * di + smoothing * smoothing)
-            grads = [grads[0] + dr * scale, grads[1] + di * scale]
-        for ri in range(2):
-            g_ref[it, i, ri] = grads[ri]
-            ag_ref[it, i, me, ri] = grads[ri].astype(bf16)
-        gg_ref[...] += grads[0] * grads[0] + grads[1] * grads[1]
+            diff = [-alpha * (tv_ref[i, t] - g_ref[0, i, t]) for t in range(3)]
+            main = diff[0] * diff[0] + diff[1] * diff[1]
+            rest = diff[2] * diff[2]
+            rest = rest + pltpu.roll(rest, HALF, 1)
+            for t, modulus in enumerate((main, main, rest)):
+                scale = (-2.0 * tv_weight) / jnp.sqrt(modulus + smoothing * smoothing)
+                grads[t] = grads[t] + diff[t] * scale
+        square = None
+        for t in range(3):
+            g_ref[it, i, t] = grads[t]
+            ag_ref[it, i, me, t] = grads[t].astype(bf16)
+            square = grads[t] * grads[t] if square is None else square + grads[t] * grads[t]
+        gg_ref[...] += square
         for k in range(1, n):
             ag_copy(it, i, k).start()
         if it == 0:
@@ -328,10 +398,10 @@
         e, x = i // readout, lax.rem(i, readout)
         for k in range(1, n):
             ag_in(it, i, k).wait_recv()
-        vr, vi = [
-            jnp.concatenate([ag_ref[it, i, b, ri] for b in range(n)], axis=0).astype(f32)
-            for ri in range(2)
-        ]
+        vr, vi = unpacked(*[
+            jnp.concatenate([ag_ref[it, i, b, t] for b in range(n)], axis=0).astype(f32)
+            for t in range(3)
+        ])
         prods = []
         for c in range(coils):
             cr, ci = coil_of(c, x)
@@ -388,7 +458,9 @@
         for s in range(1, n * nphase * nenc):
             total = total + ar_ref[it, s]
         gg, ee = total[0:1, 0:1], total[1:2, 0:1]
-        return gg / (ee + 4.0 * tv_weight / smoothing * gg + 1e-06)
+        alpha = gg / (ee + 4.0 * tv_weight / smoothing * gg + 1e-06)
+        a_ref[it] = jnp.broadcast_to(alpha, a_ref.shape[1:])
+        return alpha
 
     def finish_sends(it):
         @pl.loop(0, pieces)
@@ -419,7 +491,19 @@
             def _():
                 forward(it, s - 2 * LAG)
 
-    @pl.loop(0, pieces)
+    load_k(0).wait()
+
+    @pl.loop(0, readout)
+    def _(i):
+        transform(i, None)
+
+    pl.semaphore_wait(barrier, len(offsets))
+    for k in range(1, n):
+        coil_z(k).start()
+    for e in range(1, encs):
+        load_k(e).wait()
+
+    @pl.loop(readout, pieces)
     def _(i):
         transform(i, None)
 
@@ -430,7 +514,6 @@
     for k in range(1, n):
         coil_x(k, across).wait_recv()
         coil_c(k, across, 1).start()
-    mine.wait()
     partner = wrap(en + 1, nenc)
     for k in range(1, n):
         coil_c(k, ph * nenc + partner, 0).wait_recv()
@@ -440,21 +523,7 @@
     alpha0 = step_size(0)
     finish_sends(0)
     sweep(1, alpha0)
-    alpha1 = step_size(1)
-
-    for ri in range(2):
-        for i in range(pieces):
-            img_ref[ri, 0, i // readout, i % readout] = (
-                -alpha0 * g_ref[0, i, ri] - alpha1 * g_ref[1, i, ri]
-            )
-
-    @pl.loop(0, pieces)
-    def _(i):
-        e, x = i // readout, lax.rem(i, readout)
-        for c in range(coils):
-            r = c * readout + x
-            for ri in range(2):
-                res_ref[ri, 0, e, r] = res_ref[ri, 0, e, r] - alpha1 * e_ref[i, c, ri]
+    step_size(1)
 
     finish_sends(1)
     for k in range(1, n):
@@ -478,29 +547,34 @@
     f32, bf16 = jnp.float32, jnp.bfloat16
     dma = pltpu.SemaphoreType.DMA
     vmem = pl.BlockSpec(memory_space=pltpu.VMEM)
-    return pl.pallas_call(
+    anywhere = pl.BlockSpec(memory_space=pl.ANY)
+    left, steps, grads, alphas = pl.pallas_call(
         functools.partial(fused, (n, nphase, nenc)),
         out_shape=[
-            jax.ShapeDtypeStruct((2, 1, encs, readout, depth, lines), f32),
-            jax.ShapeDtypeStruct(kspace_data.shape, f32),
+            KEEP(kspace_data.shape, f32),
+            KEEP((pieces, coils, 2, slices, lines), f32),
+            KEEP((ITERS, pieces, 3, depth, 2 * HALF), f32),
+            KEEP((ITERS, 8, 128), f32),
         ],
-        in_specs=[vmem] * 7,
-        out_specs=[vmem] * 2,
+        in_specs=[anywhere] * 3 + [vmem] * 4,
+        out_specs=[vmem] * 4,
         scratch_shapes=[
-            pltpu.VMEM((n, 2, coils, readout, depth, lines), bf16),
+            pltpu.VMEM(kspace_data.shape, bf16),
+            pltpu.VMEM(coil_maps.shape, bf16),
+            pltpu.VMEM(sampling.shape, jnp.int32),
+            pltpu.VMEM((coils * n, 3, depth, 2 * HALF), bf16),
+            pltpu.VMEM((n, coils, readout, 3, depth, 2 * HALF), bf16),
             pltpu.VMEM((encs, slices, lines), f32),
             pltpu.VMEM((pieces, coils, 2, slices, lines), f32),
-            pltpu.VMEM((pieces, coils, 2, slices, lines), f32),
-            pltpu.VMEM((ITERS, pieces, n, 2, depth, lines), bf16),
-            pltpu.VMEM((ITERS, pieces, n - 1, 2, depth, lines), bf16),
-            pltpu.VMEM((pieces, n, 2, depth, lines), f32),
-            pltpu.VMEM((ITERS, pieces, n, 2, depth, lines), bf16),
-            pltpu.VMEM((ITERS, pieces, 2, depth, lines), f32),
-            pltpu.VMEM((pieces, 2, depth, lines), f32),
+            pltpu.VMEM((ITERS, pieces, n, 3, depth, 2 * HALF), bf16),
+            pltpu.VMEM((ITERS, pieces, n - 1, 3, depth, 2 * HALF), bf16),
+            pltpu.VMEM((pieces, n, 3, depth, 2 * HALF), f32),
+            pltpu.VMEM((ITERS, pieces, n, 3, depth, 2 * HALF), bf16),
+            pltpu.VMEM((pieces, 3, depth, 2 * HALF), f32),
             pltpu.VMEM((ITERS, group, 8, 128), f32),
-            pltpu.VMEM((depth, lines), f32),
+            pltpu.VMEM((depth, 2 * HALF), f32),
             pltpu.VMEM((slices, lines), f32),
-            dma,
+            dma((2 + encs,)),
             dma((n - 1,)),
             dma((n - 1,)),
             dma((n - 1,)),
@@ -517,9 +591,20 @@
             dma((ITERS, group - 1)),
         ],
         compiler_params=pltpu.CompilerParams(
-            collective_id=0, has_side_effects=True, vmem_limit_bytes=60 * 1024 * 1024
+            collective_id=0, has_side_effects=True, vmem_limit_bytes=LIMIT
         ),
     )(kspace_data, coil_maps, sampling, jnp.asarray(cy), jnp.asarray(sy), jnp.asarray(inv), jnp.asarray(fwd))
+    return pl.pallas_call(
+        finish,
+        out_shape=[
+            jax.ShapeDtypeStruct((2, 1, encs, readout, depth, lines), f32),
+            jax.ShapeDtypeStruct(kspace_data.shape, f32),
+        ],
+        in_specs=[vmem] * 4,
+        out_specs=[vmem, anywhere],
+        scratch_shapes=[pltpu.VMEM(kspace_data.shape, f32), dma((2, encs))],
+        compiler_params=pltpu.CompilerParams(vmem_limit_bytes=TAIL_LIMIT),
+    )(left, steps, grads, alphas)
 
 
 def chosen(shape, kspace_data, coil_maps, sampling):
@@ -531,6 +616,7 @@
         and readout == shape["phase"] * shape["enc"]
         and kspace_data.shape[3] % readout == 0
         and depth % 16 == 0
+        and coil_maps.shape[4] == 3 * HALF
         and shape["slab"] > 1
     )
     if fits:

time: 96.7 us -> 81.6 us (0.84)
  Pallas kernels: 88 us -> 76.5 us
  local copies, waits for them, and re-layouts: 7.97 us -> 4.2 us
    pallas_call x1 -> x2, Pallas kernels: 88 us -> 76.5 us  [the longest x1 72.7 us: fused_body(): pl.pallas_call(functools.partial(fused, (n, nphase, nenc)), out_shape=[KE...]
    unnamed x2 -> x10, local copies, waits for them, and re-layouts: 7.97 us -> 4.2 us
where the time goes in v2:
time: 81.6 us; the launch traced here: 81.3 us
  Pallas kernels  76.5 us (94%)
  local copies, waits for them, and re-layouts  4.2 us (5%)
    pallas_call x1, Pallas kernels, fused_body(): pl.pallas_call(functools.partial(fused, (n, nphase, nenc)), out_shape=[KE...  72.7 us
    unnamed x10, local copies, waits for them, and re-layouts  4.2 us
    pallas_call x1, Pallas kernels, fused_body(): pl.pallas_call(finish, out_shape=[jax.ShapeDtypeStruct((2, 1, encs, reado...  3.74 us

profile of v2, /device:TPU:0, one launch (start us, length us, event | category | flops | bytes accessed | tf_op | source)
XLA Modules:
  0.0 81.3 jit_solution(18207391277201375474)
XLA Ops:
  0.6 0.0 copy-start
  0.6 0.9 %copy-done = s32[1,2,64,192]{3,2,1,0:T(8,128)S(1)} copy-done((s32[1,2,64,192]{3,2,1,0:T(8,128)S(1)}, s32[1,2,64,192]{3,2,1,0:T(8,128)}, u32[]{:S(2)}) %copy-start) | copy-done | bytes 98328
  1.5 0.0 copy-start.1
  1.5 0.9 %copy-done.1 = bf16[192,192]{1,0:T(8,128)(2,1)S(1)} copy-done((bf16[192,192]{1,0:T(8,128)(2,1)S(1)}, bf16[192,192]{1,0:T(8,128)(2,1)}, u32[]{:S(2)}) %copy-start.1) | copy-done | bytes 73752
  2.4 0.0 copy-start.2
  2.4 0.9 %copy-done.2 = bf16[192,192]{1,0:T(8,128)(2,1)S(1)} copy-done((bf16[192,192]{1,0:T(8,128)(2,1)S(1)}, bf16[192,192]{1,0:T(8,128)(2,1)}, u32[]{:S(2)}) %copy-start.2) | copy-done | bytes 73752
  3.3 0.0 copy-start.3
  3.3 0.8 copy-done.3
  4.1 0.0 copy-start.4
  4.1 0.8 copy-done.4
  4.8 72.7 %shard_map.86 = (f32[2,1,2,24,64,192]{5,4,3,2,1,0:T(8,128)S(1)}, f32[8,6,2,64,192]{4,3,2,1,0:T(8,128)S(1)}, f32[2,8,3,16,128]{4,3,2,1,0:T(8,128)S(1)}, f32[2,8,128]{2,1,0:T(8,128)S(1)}) custom-call(bf16[2,1,2,24,64,192]{5,4,3,2,1,0:T(8,128)(2,1)} %k_hbm.1, bf16[2,24,4,16,192]{4,3,2,1,0:T(8,128)(2,1)} %coil_hbm.1, s32[1,2,64,192]{3,2,1,0:T(8,128)S(1)} %copy-done, ...), custom_call_target="tpu_custom_call" | custom-call | tf_op jit(solution)/shard_map/pallas_call | solution.py:551
  77.6 3.7 %shard_map.87 = (f32[2,1,2,4,16,192]{5,4,3,2,1,0:T(8,128)}, f32[2,1,2,24,64,192]{5,4,3,2,1,0:T(8,128)}) custom-call(f32[2,1,2,24,64,192]{5,4,3,2,1,0:T(8,128)S(1)} %get-tuple-element.6.r_ref, f32[8,6,2,64,192]{4,3,2,1,0:T(8,128)S(1)} %get-tuple-element.7.e_ref, f32[2,8,3,16,128]{4,3,2,1,0:T(8,128)S(1)} %get-tuple-element.8.g_ref, ...), custom_call_target="tpu_custom_call" | custom-call | tf_op jit(solution)/shard_map/pallas_call | solution.py:597
Async XLA Ops:
  0.6 0.9 %copy-start = (s32[1,2,64,192]{3,2,1,0:T(8,128)S(1)}, s32[1,2,64,192]{3,2,1,0:T(8,128)}, u32[]{:S(2)}) copy-start(s32[1,2,64,192]{3,2,1,0:T(8,128)} %samp_hbm.1) | copy-start | bytes 294916
  1.5 0.9 %copy-start.1 = (bf16[192,192]{1,0:T(8,128)(2,1)S(1)}, bf16[192,192]{1,0:T(8,128)(2,1)}, u32[]{:S(2)}) copy-start(bf16[192,192]{1,0:T(8,128)(2,1)} %constant.9.clone.sy_ref) | copy-start | bytes 221188
  2.4 0.9 %copy-start.2 = (bf16[192,192]{1,0:T(8,128)(2,1)S(1)}, bf16[192,192]{1,0:T(8,128)(2,1)}, u32[]{:S(2)}) copy-start(bf16[192,192]{1,0:T(8,128)(2,1)} %constant.8.clone.cy_ref) | copy-start | bytes 221188
  3.3 0.8 copy-start.3
  4.1 0.8 copy-start.4

commit v3 on v2

--- a/solution.py
+++ b/solution.py
@@ -140,10 +140,11 @@
 
 
 MESH = pl.DeviceIdType.MESH
-LAG = 3
+LAG, MIDDLE, LAST = 3, 5, 7
 HALF = 64
 KEEP = pltpu.VMEM
-LIMIT = 40 * 1024 * 1024
+VMEM_BYTES = 67043328
+SPARE = 7000000
 TAIL_LIMIT = 40 * 1024 * 1024
 
 
@@ -202,10 +203,10 @@
             out(ri, e).wait()
 
 
-def fused(sizes, k_hbm, coil_hbm, samp_hbm, cy_ref, sy_ref, ti_ref, tf_ref, res_ref, e_ref, g_ref,
+def fused(sizes, k_hbm, coil_hbm, samp_hbm, cy_hbm, sy_hbm, ti_hbm, tf_hbm, res_ref, e_ref, g_ref,
           a_ref, k_ref, coil_ref, samp_ref, pack_ref,
           rows_ref, mask_ref, q_ref, rs_ref, rr_ref, own_ref, ag_ref, tv_ref,
-          ar_ref, gg_ref, ee_ref,
+          ar_ref, gg_ref, ee_ref, cy_ref, sy_ref, ti_ref, tf_ref,
           in_sem, cz_send, cz_recv, cx_send, cx_recv, cc_send, cc_recv,
           rs_send, rs_recv, ag_send, ag_recv, tv_send, tv_recv, ar_send, ar_recv):
     n, nphase, nenc = sizes
@@ -273,8 +274,16 @@
 
     load_coil = pltpu.make_async_copy(coil_hbm, coil_ref, in_sem.at[0])
     load_samp = pltpu.make_async_copy(samp_hbm, samp_ref, in_sem.at[1])
+    tables = [
+        pltpu.make_async_copy(src, dst, in_sem.at[2 + encs + t])
+        for t, (src, dst) in enumerate(
+            ((cy_hbm, cy_ref), (sy_hbm, sy_ref), (ti_hbm, ti_ref), (tf_hbm, tf_ref))
+        )
+    ]
     load_coil.start()
     load_samp.start()
+    for table in tables:
+        table.start()
     for e in range(encs):
         load_k(e).start()
     load_coil.wait()
@@ -293,6 +302,8 @@
                 rows_ref[me, c, x, t] = part.astype(bf16)
 
     load_samp.wait()
+    for table in tables:
+        table.wait()
     mask_ref[...] = samp_ref[0].astype(f32)
     gg_ref[...] = jnp.zeros_like(gg_ref)
     ee_ref[...] = jnp.zeros_like(ee_ref)
@@ -335,15 +346,34 @@
             rs_send.at[i, k - 1], rs_recv.at[i, k - 1], rel(k, 0, 0),
         )
 
-    def ag_copy(it, i, k):
+    beside = me + 1 - 2 * lax.rem(me, 2)
+    opposite = wrap(me + 2, n)
+    near, over = wrap(beside - me, n), 2
+
+    def ag_send_to(it, i, block, which):
+        at = ag_ref.at[it, i, block]
         return remote(
-            ag_ref.at[it, i, me], ag_ref.at[it, i, me],
-            ag_send.at[i, k - 1], ag_recv.at[i, k - 1], rel(k, 0, 0),
+            at, at, ag_send.at[i, which], ag_recv.at[i, which],
+            rel(over if which == 1 else near, 0, 0),
         )
 
-    def ag_in(it, i, k):
-        at = ag_ref.at[it, i, wrap(me - k, n)]
-        return remote(at, at, ag_send.at[i, k - 1], ag_recv.at[i, k - 1], rel(k, 0, 0))
+    def ag_near(it, i):
+        return ag_send_to(it, i, me, 0)
+
+    def ag_near_in(it, i):
+        return ag_send_to(it, i, beside, 0)
+
+    def ag_over(it, i):
+        return ag_send_to(it, i, me, 1)
+
+    def ag_over_in(it, i):
+        return ag_send_to(it, i, opposite, 1)
+
+    def ag_relay(it, i):
+        return ag_send_to(it, i, opposite, 2)
+
+    def ag_relay_in(it, i):
+        return ag_send_to(it, i, wrap(beside + 2, n), 2)
 
     def tv_copy(i):
         return remote(g_ref.at[0, i], tv_ref.at[i], tv_send.at[i], tv_recv.at[i], rel(0, 1, 0))
@@ -389,15 +419,15 @@
             ag_ref[it, i, me, t] = grads[t].astype(bf16)
             square = grads[t] * grads[t] if square is None else square + grads[t] * grads[t]
         gg_ref[...] += square
-        for k in range(1, n):
-            ag_copy(it, i, k).start()
+        ag_over(it, i).start()
+        ag_near(it, i).start()
         if it == 0:
             tv_copy(i).start()
 
     def forward(it, i):
         e, x = i // readout, lax.rem(i, readout)
-        for k in range(1, n):
-            ag_in(it, i, k).wait_recv()
+        ag_near_in(it, i).wait_recv()
+        ag_relay_in(it, i).wait_recv()
         vr, vi = unpacked(*[
             jnp.concatenate([ag_ref[it, i, b, t] for b in range(n)], axis=0).astype(f32)
             for t in range(3)
@@ -467,29 +497,65 @@
         def _(i):
             for k in range(1, n):
                 rs_copy(it, i, k).wait_send()
-                ag_copy(it, i, k).wait_send()
+            ag_over(it, i).wait_send()
+            ag_near(it, i).wait_send()
+            ag_relay(it, i).wait_send()
             if it == 0:
                 tv_copy(i).wait_send()
 
         for j in range(len(offsets)):
             ar_copy(it, j).wait_send()
 
+    partner = wrap(en + 1, nenc)
+    beyond = wrap(ph + 1, nphase)
+
+    def piece(s):
+        e, j = lax.rem(s, encs), s // encs
+        x = wrap(ph + j // nenc, nphase) * nenc + wrap(en + lax.rem(j, nenc), nenc)
+        return e * readout + x
+
+    def coils_ready(s):
+        @pl.when(s == encs)
+        def _():
+            for k in range(1, n):
+                coil_c(k, ph * nenc + partner, 0).wait_recv()
+
+        @pl.when(s == nenc * encs)
+        def _():
+            for k in range(1, n):
+                coil_x(k, across).wait_recv()
+                coil_c(k, across, 1).start()
+
+        @pl.when(s == (nenc + 1) * encs)
+        def _():
+            for k in range(1, n):
+                coil_c(k, beyond * nenc + partner, 1).wait_recv()
+
     def sweep(it, alpha):
-        @pl.loop(0, pieces + 2 * LAG)
+        @pl.loop(0, pieces + LAST)
         def _(s):
             @pl.when(s < pieces)
             def _():
+                p = piece(s)
                 if it > 0:
-                    transform(s, alpha)
-                combine(it, s)
+                    transform(p, alpha)
+                else:
+                    coils_ready(s)
+                combine(it, p)
 
             @pl.when((s >= LAG) & (s < pieces + LAG))
             def _():
-                reduce(it, s - LAG, alpha)
-
-            @pl.when(s >= 2 * LAG)
+                reduce(it, piece(s - LAG), alpha)
+
+            @pl.when((s >= MIDDLE) & (s < pieces + MIDDLE))
             def _():
-                forward(it, s - 2 * LAG)
+                p = piece(s - MIDDLE)
+                ag_over_in(it, p).wait_recv()
+                ag_relay(it, p).start()
+
+            @pl.when(s >= LAST)
+            def _():
+                forward(it, piece(s - LAST))
 
     load_k(0).wait()
 
@@ -507,17 +573,14 @@
     def _(i):
         transform(i, None)
 
-    for k in range(1, n):
+    nearest = [sorted(range(1, n), key=lambda k: abs((m - k) % n - m)) for m in range(n)]
+    for j in range(n - 1):
+        k = nearest[0][j]
+        for m in range(1, n):
+            k = jnp.where(me == m, nearest[m][j], k)
         coil_z_in(k).wait_recv()
         coil_x(k, quarter).start()
         coil_c(k, quarter, 0).start()
-    for k in range(1, n):
-        coil_x(k, across).wait_recv()
-        coil_c(k, across, 1).start()
-    partner = wrap(en + 1, nenc)
-    for k in range(1, n):
-        coil_c(k, ph * nenc + partner, 0).wait_recv()
-        coil_c(k, wrap(ph + 1, nphase) * nenc + partner, 1).wait_recv()
 
     sweep(0, None)
     alpha0 = step_size(0)
@@ -548,6 +611,9 @@
     dma = pltpu.SemaphoreType.DMA
     vmem = pl.BlockSpec(memory_space=pltpu.VMEM)
     anywhere = pl.BlockSpec(memory_space=pl.ANY)
+    stay = pl.BlockSpec(memory_space=pltpu.HBM)
+    wide = -(-lines // 128) * 128
+    kept = 4 * (2 * encs * row_count * slices * wide * 2 + ITERS * (pieces * 3 * depth * 128 + 1024))
     left, steps, grads, alphas = pl.pallas_call(
         functools.partial(fused, (n, nphase, nenc)),
         out_shape=[
@@ -556,7 +622,7 @@
             KEEP((ITERS, pieces, 3, depth, 2 * HALF), f32),
             KEEP((ITERS, 8, 128), f32),
         ],
-        in_specs=[anywhere] * 3 + [vmem] * 4,
+        in_specs=[stay] * 7,
         out_specs=[vmem] * 4,
         scratch_shapes=[
             pltpu.VMEM(kspace_data.shape, bf16),
@@ -574,7 +640,11 @@
             pltpu.VMEM((ITERS, group, 8, 128), f32),
             pltpu.VMEM((depth, 2 * HALF), f32),
             pltpu.VMEM((slices, lines), f32),
-            dma((2 + encs,)),
+            pltpu.VMEM((lines, lines), bf16),
+            pltpu.VMEM((lines, lines), bf16),
+            pltpu.VMEM((2 * slices, 2 * slices), bf16),
+            pltpu.VMEM((2 * slices, 2 * slices), bf16),
+            dma((6 + encs,)),
             dma((n - 1,)),
             dma((n - 1,)),
             dma((n - 1,)),
@@ -591,7 +661,7 @@
             dma((ITERS, group - 1)),
         ],
         compiler_params=pltpu.CompilerParams(
-            collective_id=0, has_side_effects=True, vmem_limit_bytes=LIMIT
+            collective_id=0, has_side_effects=True, vmem_limit_bytes=(VMEM_BYTES - kept - SPARE) // 1024 * 1024
         ),
     )(kspace_data, coil_maps, sampling, jnp.asarray(cy), jnp.asarray(sy), jnp.asarray(inv), jnp.asarray(fwd))
     return pl.pallas_call(
@@ -617,7 +687,7 @@
         and kspace_data.shape[3] % readout == 0
         and depth % 16 == 0
         and coil_maps.shape[4] == 3 * HALF
-        and shape["slab"] > 1
+        and shape["slab"] == 4
     )
     if fits:
         return fused_body(shape, kspace_data, coil_maps, sampling)

time: 81.6 us -> 74 us (0.907)
  local copies, waits for them, and re-layouts: 4.2 us -> 0 us
  Pallas kernels: 76.5 us -> 73.2 us
    unnamed x10 -> x0, local copies, waits for them, and re-layouts: 4.2 us -> none
    pallas_call x1, Pallas kernels: 72.7 us -> 69.5 us  [fused_body(): pl.pallas_call(functools.partial(fused, (n, nphase, nenc)), out_shape=[KE...]
where the time goes in v3:
time: 74 us; the launch traced here: 73.9 us
  Pallas kernels  73.2 us (99%)
    pallas_call x1, Pallas kernels, fused_body(): pl.pallas_call(functools.partial(fused, (n, nphase, nenc)), out_shape=[KE...  69.5 us
    pallas_call x1, Pallas kernels, fused_body(): pl.pallas_call(finish, out_shape=[jax.ShapeDtypeStruct((2, 1, encs, reado...  3.74 us

profile of v3, /device:TPU:0, one launch (start us, length us, event | category | flops | bytes accessed | tf_op | source)
XLA Modules:
  0.0 73.9 jit_solution(10881405783152209772)
XLA Ops:
  0.6 69.5 %shard_map.86 = (f32[2,1,2,24,64,192]{5,4,3,2,1,0:T(8,128)S(1)}, f32[8,6,2,64,192]{4,3,2,1,0:T(8,128)S(1)}, f32[2,8,3,16,128]{4,3,2,1,0:T(8,128)S(1)}, f32[2,8,128]{2,1,0:T(8,128)S(1)}) custom-call(bf16[2,1,2,24,64,192]{5,4,3,2,1,0:T(8,128)(2,1)} %k_hbm.1, bf16[2,24,4,16,192]{4,3,2,1,0:T(8,128)(2,1)} %coil_hbm.1, s32[1,2,64,192]{3,2,1,0:T(8,128)} %samp_hbm.1, ...), custom_call_target="tpu_custom_call" | custom-call | tf_op jit(solution)/shard_map/pallas_call | solution.py:617
  70.1 3.7 %shard_map.87 = (f32[2,1,2,4,16,192]{5,4,3,2,1,0:T(8,128)}, f32[2,1,2,24,64,192]{5,4,3,2,1,0:T(8,128)}) custom-call(f32[2,1,2,24,64,192]{5,4,3,2,1,0:T(8,128)S(1)} %get-tuple-element.6.r_ref, f32[8,6,2,64,192]{4,3,2,1,0:T(8,128)S(1)} %get-tuple-element.7.e_ref, f32[2,8,3,16,128]{4,3,2,1,0:T(8,128)S(1)} %get-tuple-element.8.g_ref, ...), custom_call_target="tpu_custom_call" | custom-call | tf_op jit(solution)/shard_map/pallas_call | solution.py:667
